TPU v7x, 32 devices: a whole 2x2x4 slice. The times are simulated.
32 devices in a mesh: groups: 2 (over y), seq: 4 (over z), exp: 2 (over x), tp: 2 (over core).
Axes of the slice: x: 2, y: 2, z: 4, core: 2. Of those that a mesh axis runs over, the one named last changes fastest.
Arguments:
- attn_query: bfloat16 [2048, 1152], P(('groups', 'seq'), ('exp', 'tp')), parts along dimension 0, may hold values from -6 to 6
- fresh_keys: bfloat16 [2048, 1152], P(('groups', 'seq'), ('exp', 'tp')), parts along dimension 0, may hold values from -6 to 6
- fresh_values: bfloat16 [2048, 1152], P(('groups', 'seq'), ('exp', 'tp')), parts along dimension 0, may hold values from -6 to 6
- stale_keys: bfloat16 [2048, 1152], P(('groups', 'seq'), ('exp', 'tp')), parts along dimension 0, may hold values from -6 to 6
- stale_values: bfloat16 [2048, 1152], P(('groups', 'seq'), ('exp', 'tp')), parts along dimension 0, may hold values from -6 to 6
- block_flags: int32 [16], P(('groups', 'seq')), parts along dimension 0, may hold values 0 or 1
- moe_tokens: bfloat16 [4096, 1152], P(('groups', 'seq', 'exp', 'tp')), parts along dimension 0, may hold values from -6 to 6
- expert_ids: int32 [4096, 2], P(('groups', 'seq', 'exp', 'tp')), parts along dimension 0, may hold values from 0 to 3, all different within a row; in each aligned block of 128 rows (0 to 127, 128 to 255, ...) at most 80 rows name the same one
- gate_weights: float32 [4096, 2], P(('groups', 'seq', 'exp', 'tp')), parts along dimension 0, may hold values from 0.25 to 1
- up_weight: bfloat16 [4, 1152, 4608], P('seq', None, ('exp', 'tp')), may hold values from -0.1875 to 0.1875
- up_bias: float32 [4, 4608], P('seq', ('exp', 'tp')), may hold values from -3 to 3
- down_weight: bfloat16 [4, 4608, 1152], P('seq', ('exp', 'tp')), may hold values from -0.09375 to 0.09375
- down_bias: float32 [4, 1152], P('seq'), may hold values from -2 to 2
Outputs:
- attn_out: bfloat16 [2048, 1152], P(('groups', 'seq'), ('exp', 'tp')), parts along dimension 0
- moe_out: bfloat16 [4096, 1152], P(('groups', 'seq', 'exp', 'tp')), parts along dimension 0
There are 2 independent parts, one for each index of `groups`. A program takes and returns all parts, laid end to end along the dimension named above; an argument that names none is the same for every part. Nothing has to cross between parts.
Inputs may be any that keep to these rules, and one draw needn't show every extreme that they name: `expert_ids`: the 2 ids of a token differ. In the rows of one device no expert is named more than 80 times, and in every draw some expert is named exactly 80 times in some device's rows.
All inputs are finite; a program needn't handle non-finite values. No bound on the sum of `block_flags` on one device may be relied on, other than what follows from the above.
Results may differ from a plain program's by a relative error of at most 0.014.
Values may be sent and summed in bfloat16 or wider, within the bound.
A program may use at most 64 MiB of HBM per device.

v0:
```python
import math
import jax
import jax.numpy as jnp
from jax import lax
from jax.sharding import PartitionSpec as P

HD = 72


def over_all_2(share, axis, dim, apply):
    everything = lax.all_gather(share, axis, axis=dim, tiled=True)
    return apply(everything, jnp.int32(0))


def attention_part(attn_query, fresh_keys, fresh_values, stale_keys, stale_values, block_flags):
    length = attn_query.shape[0]
    heads_here = attn_query.shape[1] // HD
    row_flags = (jnp.repeat(block_flags, length // block_flags.shape[0]) == 1)[:, None]
    keys = jnp.where(row_flags, fresh_keys, stale_keys)
    values = jnp.where(row_flags, fresh_values, stale_values)
    queries = attn_query.reshape(length, heads_here, HD)
    scale = 1.0 / math.sqrt(HD)
    initial = (
        jnp.full((heads_here, length), -1e30, jnp.float32),
        jnp.zeros((heads_here, length), jnp.float32),
        jnp.zeros((heads_here, length, HD), jnp.float32),
    )
    carry = initial
    piece = (
        lax.all_gather(keys, "seq", axis=0, tiled=True),
        lax.all_gather(values, "seq", axis=0, tiled=True),
    )
    count = piece[0].shape[0]
    width = math.gcd(count, 512)
    key_blocks = piece[0].reshape(count // width, width, heads_here, HD)
    value_blocks = piece[1].reshape(count // width, width, heads_here, HD)

    def advance(state, blocks):
        highest, totals, weighted = state
        key_block, value_block = blocks
        scores = (
            jnp.einsum("qhd,khd->hqk", queries, key_block, preferred_element_type=jnp.float32)
            * scale
        )
        new_high = jnp.maximum(highest, jnp.max(scores, axis=-1))
        rescale = jnp.exp(highest - new_high)
        probs = jnp.exp(scores - new_high[:, :, None])
        totals = totals * rescale + jnp.sum(probs, axis=-1)
        weighted = weighted * rescale[:, :, None] + jnp.einsum(
            "hqk,khd->hqd",
            probs.astype(jnp.bfloat16),
            value_block,
            preferred_element_type=jnp.float32,
        )
        return ((new_high, totals, weighted), None)

    carry, unused = lax.scan(advance, carry, (key_blocks, value_blocks))
    highest, totals, weighted = carry
    mixed = weighted / totals[:, :, None]
    return jnp.transpose(mixed, (1, 0, 2)).reshape(length, heads_here * HD).astype(jnp.bfloat16)


def expert_part(moe_tokens, expert_ids, gate_weights, up_weight, up_bias, down_weight, down_bias):
    tokens_here, width = moe_tokens.shape
    choose = expert_ids.shape[1]
    number = lax.axis_size("seq") * up_weight.shape[0]
    capacity = 5 * tokens_here // (2 * number)
    flat_ids = expert_ids.reshape(-1)
    hits = (flat_ids[:, None] == jnp.arange(number, dtype=jnp.int32)[None, :]).astype(jnp.int32)
    before = jnp.cumsum(hits, axis=0) - hits
    place = jnp.sum(before * hits, axis=1)
    slot = flat_ids * capacity + place
    slot_pairs = slot.reshape(tokens_here, choose)
    table = jnp.sum(
        (
            slot_pairs[None, :, :] == jnp.arange(number * capacity, dtype=jnp.int32)[:, None, None]
        ).astype(jnp.int32),
        axis=-1,
    )
    buffer = jnp.dot(
        table.astype(jnp.bfloat16), moe_tokens, preferred_element_type=jnp.float32
    ).astype(jnp.bfloat16)
    buffer = buffer.reshape(number, capacity, width)
    received = lax.all_to_all(buffer, "seq", split_axis=0, concat_axis=0, tiled=True)
    sources = received.shape[0]
    count = received.shape[1]
    flat_rows = received.reshape(sources * count, width)
    chip_rows = lax.all_gather(flat_rows, "tp", axis=0, tiled=True)

    def project(piece):
        return jax.nn.gelu(
            jnp.dot(chip_rows, piece[0], preferred_element_type=jnp.float32) + piece[1]
        ).astype(jnp.bfloat16)

    hidden = over_all_2(
        (up_weight[0], up_bias[0][None, :].astype(jnp.bfloat16)),
        "exp",
        1,
        lambda piece, start: project((piece[0], piece[1].astype(jnp.float32))),
    )
    down_whole = lax.all_gather(down_weight[0], "exp", axis=0, tiled=True)
    summed = lax.psum_scatter(
        jnp.dot(hidden, down_whole, preferred_element_type=jnp.float32).astype(jnp.bfloat16),
        "tp",
        scatter_dimension=0,
        tiled=True,
    ).astype(jnp.float32)
    result = (summed + down_bias[0][None, :]).astype(jnp.bfloat16).reshape(sources, count, width)
    returned = lax.all_to_all(result, "seq", split_axis=0, concat_axis=0, tiled=True)
    flat_out = returned.reshape(number * capacity, width)
    picked = flat_out[slot].reshape(tokens_here, choose, width).astype(jnp.float32)
    combined = jnp.sum(picked * gate_weights[:, :, None], axis=1)
    return combined.astype(jnp.bfloat16)


def local(
    attn_query,
    fresh_keys,
    fresh_values,
    stale_keys,
    stale_values,
    block_flags,
    moe_tokens,
    expert_ids,
    gate_weights,
    up_weight,
    up_bias,
    down_weight,
    down_bias,
):
    attn_out = attention_part(
        attn_query, fresh_keys, fresh_values, stale_keys, stale_values, block_flags
    )
    moe_out = expert_part(
        moe_tokens, expert_ids, gate_weights, up_weight, up_bias, down_weight, down_bias
    )
    return (attn_out, moe_out)


def solution(mesh):
    in_specs = (
        P(("groups", "seq"), ("exp", "tp")),
        P(("groups", "seq"), ("exp", "tp")),
        P(("groups", "seq"), ("exp", "tp")),
        P(("groups", "seq"), ("exp", "tp")),
        P(("groups", "seq"), ("exp", "tp")),
        P(("groups", "seq")),
        P(("groups", "seq", "exp", "tp"), None),
        P(("groups", "seq", "exp", "tp"), None),
        P(("groups", "seq", "exp", "tp"), None),
        P("seq", None, ("exp", "tp")),
        P("seq", ("exp", "tp")),
        P("seq", ("exp", "tp"), None),
        P("seq", None),
    )
    out_specs = (P(("groups", "seq"), ("exp", "tp")), P(("groups", "seq", "exp", "tp"), None))
    return jax.shard_map(local, mesh=mesh, in_specs=in_specs, out_specs=out_specs, check_vma=False)
```

profile of v0, /device:TPU:0, one launch (start us, length us, event | category | flops | bytes accessed | tf_op | source)
XLA Modules:
  0.0 262.1 jit_solution(10440550585438227936)
XLA Ops:
  7.2 0.8 copy.32
  8.3 1.2 reduce-window.6
  10.3 0.3 convolution_convert_fusion
  10.6 25.3 %all_to_all.10 = bf16[4,80,1152]{2,1,0:T(8,128)(2,1)} all-to-all(bf16[4,80,1152]{2,1,0:T(8,128)(2,1)S(1)} %bitcast.82), channel_id=1, replica_groups=mesh['groups'=2,'seq'=4,'exp'=2,'tp'=2] {'seq'}, dimensions={0} | all-to-all | bytes 1474560 | tf_op jit(solution)/shard_map/all_to_all | solution.py:84
  36.0 0.7 all-gather.8.cloned.1.call-update
  36.8 0.7 all-gather.10.cloned.1.call-update
  37.5 4.4 %all_gather.22 = bf16[1,2304]{1,0:T(2,128)(2,1)S(1)} all-gather(bf16[1,1152]{1,0:T(2,128)(2,1)S(1)} %convert_element_type.61), channel_id=1, replica_groups=mesh['groups'=2,'seq'=4,'exp'=2,'tp'=2] {'exp'}, dimensions={1}, use_global_device_ids=true | all-gather | bytes 6912 | tf_op jit(solution)/shard_map/all_gather | solution.py:11
  41.9 3.0 %all-gather.6.cloned.1.call-done = bf16[640,1152]{1,0:T(8,128)(2,1)} async-done(((bf16[320,1152]{1,0:T(8,128)(2,1)}), bf16[640,1152]{1,0:T(8,128)(2,1)}) %all-gather.6.cloned.1.call-update) | async-done | bytes 1474576 | tf_op jit(solution)/shard_map/all_gather | solution.py:88
  44.9 72.0 %all-gather.8.cloned.1.call-done = bf16[1,1152,2304]{2,1,0:T(8,128)(2,1)} async-done(((bf16[1,1152,1152]{2,1,0:T(8,128)(2,1)}), bf16[1,1152,2304]{2,1,0:T(8,128)(2,1)}) %all-gather.8.cloned.1.call-update) | async-done | bytes 5308432 | tf_op jit(solution)/shard_map/all_gather | solution.py:11
  116.9 9.6 %fusion.22 = bf16[640,2304]{1,0:T(8,128)(2,1)} fusion(bf16[640,1152]{1,0:T(8,128)(2,1)} %all-gather.6.cloned.1.call-done, bf16[1,1152,2304]{2,1,0:T(8,128)(2,1)} %all-gather.8.cloned.1.call-done, f32[2304]{0:T(1024)S(1)} %convert_reduce_fusion.1), kind=kOutput, calls=%fused_computation.30 | convolution fusion | flops 3412131840 | bytes 9741312 | tf_op jit(solution)/shard_map/dot_general | solution.py:92
  126.5 61.3 %all-gather.10.cloned.1.call-done = bf16[1,2304,1152]{2,1,0:T(8,128)(2,1)} async-done(((bf16[1,1152,1152]{2,1,0:T(8,128)(2,1)}), bf16[1,2304,1152]{2,1,0:T(8,128)(2,1)}) %all-gather.10.cloned.1.call-update) | async-done | bytes 5308432 | tf_op jit(solution)/shard_map/all_gather | solution.py:101
  187.8 8.5 %fusion.29 = bf16[640,1152]{1,0:T(8,128)(2,1)} fusion(bf16[640,2304]{1,0:T(8,128)(2,1)} %fusion.22, bf16[1,2304,1152]{2,1,0:T(8,128)(2,1)} %all-gather.10.cloned.1.call-done), kind=kOutput, calls=%fused_computation.35 | convolution fusion | flops 3398123520 | bytes 9732096 | tf_op jit(solution)/shard_map/dot_general | solution.py:103
  196.5 16.5 %all_gather.18 = bf16[1024,288]{0,1:T(8,128)(2,1)S(1)} all-gather(bf16[256,288]{0,1:T(8,128)(2,1)S(1)} %get-tuple-element.101), channel_id=1, replica_groups=mesh['groups'=2,'seq'=4,'exp'=2,'tp'=2] {'seq'}, dimensions={0}, use_global_device_ids=true | all-gather | bytes 737280 | tf_op jit(solution)/shard_map/all_gather | solution.py:30
  213.1 0.4 reshape.94
  213.5 0.9 copy.30
  214.4 16.1 %all_gather.19 = bf16[1024,288]{0,1:T(8,128)(2,1)S(1)} all-gather(bf16[256,288]{0,1:T(8,128)(2,1)S(1)} %get-tuple-element.100), channel_id=1, replica_groups=mesh['groups'=2,'seq'=4,'exp'=2,'tp'=2] {'seq'}, dimensions={0}, use_global_device_ids=true | all-gather | bytes 737280 | tf_op jit(solution)/shard_map/all_gather | solution.py:31
  230.5 0.4 reshape.96
  230.9 0.9 copy.31
  231.9 2.1 add_convert_fusion
  234.0 4.9 %all-to-all-start.1 = ((bf16[4,80,1152]{2,1,0:T(8,128)(2,1)}), bf16[4,80,1152]{2,1,0:T(8,128)(2,1)S(1)}, u32[]{:S(2)}, u32[]{:S(2)}) async-start(bf16[4,80,1152]{2,1,0:T(8,128)(2,1)} %bitcast.10), calls=%async_computation.2 | async-start | bytes 1474560 | tf_op jit(solution)/shard_map/all_to_all | solution.py:109
  238.8 6.9 %while.15 = (s32[]{:T(128)}, f32[4,256]{1,0:T(4,128)S(1)}, f32[4,256]{1,0:T(4,128)S(1)}, f32[4,256,72]{1,2,0:T(8,128)S(1)}, bf16[2,512,4,72]{1,3,2,0:T(8,128)(2,...) while((s32[]{:T(128)}, f32[4,256]{1,0:T(4,128)S(1)}, ...), condition=%wide.region_3.4_spmd.clone, body=%wide.region_0.3_spmd.clone.sunk | while | flops 155415552 | bytes 7685225 | solution.py:57
  238.8 1.5 bitcast_reduce_fusion.2
  240.4 0.4 fusion.49
  240.8 1.5 convolution_add_fusion.2
  242.3 1.5 bitcast_reduce_fusion.2
  243.8 0.4 fusion.49
  244.2 1.5 convolution_add_fusion.2
  246.0 0.7 divide_convert_fusion
  246.7 4.9 %all-to-all-done.1 = bf16[4,80,1152]{2,1,0:T(8,128)(2,1)S(1)} async-done(((bf16[4,80,1152]{2,1,0:T(8,128)(2,1)}), bf16[4,80,1152]{2,1,0:T(8,128)(2,1)S(1)}, u32[]{:S(2)}, u32[]{:S(2)}) %all-to-all-start.1) | async-done | bytes 737312 | tf_op jit(solution)/shard_map/all_to_all | solution.py:109
  251.6 1.3 gather_fusion
  252.8 0.6 reshape.103
  253.4 2.2 multiply_reduce_fusion
  (58 shorter events, 1.7 us)
Async XLA Ops:
  7.2 3.1 %copy-start = (bf16[128,1152]{1,0:T(8,128)(2,1)S(1)}, bf16[128,1152]{1,0:T(8,128)(2,1)}, u32[]{:S(2)}) copy-start(bf16[128,1152]{1,0:T(8,128)(2,1)} %param.21) | copy-start | bytes 884740
  7.2 37.7 %all-gather.6.cloned.1.call-start = ((), (), s32[]{:S(2)}) async-start(), calls=%async_computation.3 | async-start | bytes 2211840 | tf_op jit(solution)/shard_map/all_gather | solution.py:88
  36.0 1.5 copy-start.5
  36.0 80.9 %all-gather.8.cloned.1.call-start = ((), (), s32[]{:S(2)}) async-start(), calls=%async_computation.5 | async-start | bytes 7962624 | tf_op jit(solution)/shard_map/all_gather | solution.py:11
  36.7 151.0 %all-gather.10.cloned.1.call-start = ((), (), s32[]{:S(2)}) async-start(), calls=%async_computation.6 | async-start | bytes 7962624 | tf_op jit(solution)/shard_map/all_gather | solution.py:101
  37.5 194.4 %reduce-scatter.2.cloned.1.call-start = ((), (), s32[]{:S(2)}) async-start(), calls=%async_computation.4 | async-start | bytes 2211840 | tf_op jit(solution)/shard_map/reduce_scatter | solution.py:102
  126.5 69.9 %copy-start.8 = (s32[2]{0:T(128)S(1)}, s32[2]{0:T(128)}, u32[]{:S(2)}) copy-start(s32[2]{0:T(128)} %param.20) | copy-start | bytes 28
  126.5 70.0 %copy-start.1 = (bf16[256,288]{0,1:T(8,128)(2,1)S(1)}, bf16[256,288]{0,1:T(8,128)(2,1)}, u32[]{:S(2)}) copy-start(bf16[256,288]{0,1:T(8,128)(2,1)} %param.17) | copy-start | bytes 442372
  126.5 70.0 %copy-start.2 = (bf16[256,288]{0,1:T(8,128)(2,1)S(1)}, bf16[256,288]{0,1:T(8,128)(2,1)}, u32[]{:S(2)}) copy-start(bf16[256,288]{0,1:T(8,128)(2,1)} %param.19) | copy-start | bytes 442372
  126.5 70.0 %copy-start.3 = (bf16[256,288]{0,1:T(8,128)(2,1)S(1)}, bf16[256,288]{0,1:T(8,128)(2,1)}, u32[]{:S(2)}) copy-start(bf16[256,288]{0,1:T(8,128)(2,1)} %param.16) | copy-start | bytes 442372
  126.5 70.0 %copy-start.4 = (bf16[256,288]{0,1:T(8,128)(2,1)S(1)}, bf16[256,288]{0,1:T(8,128)(2,1)}, u32[]{:S(2)}) copy-start(bf16[256,288]{0,1:T(8,128)(2,1)} %param.18) | copy-start | bytes 442372
  213.1 18.7 %copy-start.6 = (f32[1,1152]{1,0:T(1,128)S(1)}, f32[1,1152]{1,0:T(1,128)}, u32[]{:S(2)}) copy-start(f32[1,1152]{1,0:T(1,128)} %param.27) | copy-start | bytes 13828
  234.0 17.6 %all-to-all-start.1 = ((bf16[4,80,1152]{2,1,0:T(8,128)(2,1)}), bf16[4,80,1152]{2,1,0:T(8,128)(2,1)S(1)}, u32[]{:S(2)}, u32[]{:S(2)}) async-start(bf16[4,80,1152]{2,1,0:T(8,128)(2,1)} %bitcast.10), calls=%async_computation.2 | async-start | bytes 1474560 | tf_op jit(solution)/shard_map/all_to_all | solution.py:109
  238.8 7.0 %copy-start.7 = (f32[128,2]{0,1:T(2,128)S(1)}, f32[128,2]{0,1:T(2,128)}, u32[]{:S(2)}) copy-start(f32[128,2]{0,1:T(2,128)} %param.23) | copy-start | bytes 3076
Sparse Core Ops, SparseCore 0:
  36.1 8.7 all-gather.5
  46.4 70.4 all-gather.7
  118.5 69.2 all-gather.9
  196.5 8.9 reduce-scatter.1
where the time goes:
time: 263 us; the launch traced here: 262 us
  waiting for transfers between devices  143 us (54%)
  blocking collectives  62.3 us (24%)
  matrix products  24.4 us (9%)
  between operations  14 us (5%)
  other arithmetic  7.3 us (3%)
  local copies, waits for them, and re-layouts  6.41 us (2%)
  starting transfers between devices  5.02 us (2%)
    all_gather x1, waiting for transfers between devices, over_all_2(): everything = lax.all_gather(share, axis, axis=dim, tiled=True)  72 us
    all_gather x1, waiting for transfers between devices, expert_part(): down_whole = lax.all_gather(down_weight[0], 'exp', axis=0, tiled=True)  61.3 us
    all_to_all x1, blocking collectives, expert_part(): lax.all_to_all(buffer, 'seq', split_axis=0, concat_axis=0, tiled=True)  25.3 us
    all_gather x1, blocking collectives, attention_part(): lax.all_gather(keys, 'seq', axis=0, tiled=True)  16.5 us
    all_gather x1, blocking collectives, attention_part(): lax.all_gather(values, 'seq', axis=0, tiled=True)  16.1 us
    dot_general x1, matrix products, project(): jnp.dot(chip_rows, piece[0], preferred_element_type=jnp.float32) + piece[1]  9.57 us
    dot_general x1, matrix products, expert_part(): jnp.dot(hidden, down_whole, preferred_element_type=jnp.float32)  8.54 us
  transfers between devices with their start and end apart: 5, of which 4 were waited for; matrix products, arithmetic and copies ran while one was open for 8% of the time, Pallas kernels for 0%

commit v1 on v0

--- a/solution.py
+++ b/solution.py
@@ -5,6 +5,14 @@
 from jax.sharding import PartitionSpec as P
 
 HD = 72
+
+
+def gather_by_exchange(value, axis, dim):
+    devices = lax.axis_size(axis)
+    repeats = [devices if d == dim else 1 for d in range(value.ndim)]
+    return lax.all_to_all(
+        jnp.tile(value, repeats), axis, split_axis=dim, concat_axis=dim, tiled=True
+    )
 
 
 def over_all_2(share, axis, dim, apply):
@@ -98,7 +106,7 @@
         1,
         lambda piece, start: project((piece[0], piece[1].astype(jnp.float32))),
     )
-    down_whole = lax.all_gather(down_weight[0], "exp", axis=0, tiled=True)
+    down_whole = gather_by_exchange(down_weight[0], "exp", 0)
     summed = lax.psum_scatter(
         jnp.dot(hidden, down_whole, preferred_element_type=jnp.float32).astype(jnp.bfloat16),
         "tp",

time: 263 us -> 240 us (0.913)
  waiting for transfers between devices: 143 us -> 17 us
  blocking collectives: 62.3 us -> 163 us
  matrix products: 24.4 us -> 18.1 us
  starting transfers between devices: 5.02 us -> 10.1 us
  local copies, waits for them, and re-layouts: 6.41 us -> 10.5 us
    all_gather x1, blocking collectives: 4.37 us -> 105 us  [over_all_2(): everything = lax.all_gather(share, axis, axis=dim, tiled=True)]
    all_gather x1, waiting for transfers between devices: 72 us -> 10.3 us  [over_all_2(): everything = lax.all_gather(share, axis, axis=dim, tiled=True)]
    all_gather x1 -> x0, waiting for transfers between devices: 61.3 us -> none  [expert_part(): down_whole = lax.all_gather(down_weight[0], 'exp', axis=0, tiled=True)]
    dot_general x1 -> x0, matrix products: 9.57 us -> none  [project(): jnp.dot(chip_rows, piece[0], preferred_element_type=jnp.float32) + piece[1]]
    all_to_all x0 -> x1, starting transfers between devices: none -> 6.33 us  [gather_by_exchange(): lax.all_to_all(jnp.tile(value, repeats), axis, split_axis=dim, concat_axi...]
    dot_general x1, matrix products: 8.54 us -> 13.7 us  [expert_part(): jnp.dot(hidden, down_whole, preferred_element_type=jnp.float32)]
    all_gather x1, waiting for transfers between devices: 2.95 us -> 0.02 us  [expert_part(): chip_rows = lax.all_gather(flat_rows, 'tp', axis=0, tiled=True)]
    another operation x2 -> x3, local copies, waits for them, and re-layouts: 0.1 us -> 2.87 us  [the longest x1 2.77 us: gather_by_exchange(): jnp.tile(value, repeats)]
  transfers between devices with their start and end apart: 5 -> 5, of which waited for: 4 -> 2; matrix products, arithmetic and copies ran while one was open for 8% -> 5% of each run, Pallas kernels for 0% -> 0%
where the time goes in v1:
time: 240 us
  blocking collectives  163 us (68%)
  matrix products  18.1 us (8%)
  waiting for transfers between devices  17 us (7%)
  between operations  14 us (6%)
  local copies, waits for them, and re-layouts  10.5 us (4%)
  starting transfers between devices  10.1 us (4%)
  other arithmetic  7.3 us (3%)
    all_gather x1, blocking collectives, over_all_2(): everything = lax.all_gather(share, axis, axis=dim, tiled=True)  105 us
    all_to_all x1, blocking collectives, expert_part(): lax.all_to_all(buffer, 'seq', split_axis=0, concat_axis=0, tiled=True)  25.6 us
    all_gather x1, blocking collectives, attention_part(): lax.all_gather(keys, 'seq', axis=0, tiled=True)  16.3 us
    all_gather x1, blocking collectives, attention_part(): lax.all_gather(values, 'seq', axis=0, tiled=True)  15.5 us
    dot_general x1, matrix products, expert_part(): jnp.dot(hidden, down_whole, preferred_element_type=jnp.float32)  13.7 us
    all_gather x1, waiting for transfers between devices, over_all_2(): everything = lax.all_gather(share, axis, axis=dim, tiled=True)  10.3 us
    all_to_all x1, starting transfers between devices, gather_by_exchange(): lax.all_to_all(jnp.tile(value, repeats), axis, split_axis=dim, concat_axi...  6.33 us
    all_to_all x1, waiting for transfers between devices, expert_part(): lax.all_to_all(result, 'seq', split_axis=0, concat_axis=0, tiled=True)  5.94 us
  transfers between devices with their start and end apart: 5, of which 2 were waited for; matrix products, arithmetic and copies ran while one was open for 5% of the time, Pallas kernels for 0%

profile of v1, /device:TPU:0, one launch (start us, length us, event | category | flops | bytes accessed | tf_op | source)
XLA Modules:
  0.0 239.9 jit_solution(4334723350687874995)
XLA Ops:
  7.2 0.8 copy.32
  8.3 1.2 reduce-window.6
  10.3 0.3 convolution_convert_fusion.1
  10.7 25.6 %all_to_all.19 = bf16[4,80,1152]{2,1,0:T(8,128)(2,1)} all-to-all(bf16[4,80,1152]{2,1,0:T(8,128)(2,1)S(1)} %bitcast.81), channel_id=1, replica_groups=mesh['groups'=2,'seq'=4,'exp'=2,'tp'=2] {'seq'}, dimensions={0} | all-to-all | bytes 1474560 | tf_op jit(solution)/shard_map/all_to_all | solution.py:92
  36.3 0.7 all-gather.6.cloned.1.call-update
  37.0 2.8 %tile.9 = bf16[2,1152,1152]{2,1,0:T(8,128)(2,1)} broadcast(bf16[1152,1152]{1,0:T(8,128)(2,1)S(1)} %bitcast.82), dimensions={1,2} | broadcast | bytes 7962624 | tf_op jit(solution)/shard_map/tile | solution.py:14
  39.8 6.3 %all-to-all-start.1 = ((bf16[2,1152,1152]{2,1,0:T(8,128)(2,1)}), bf16[2,1152,1152]{2,1,0:T(8,128)(2,1)}, u32[]{:S(2)}, u32[]{:S(2)}) async-start(bf16[2,1152,1152]{2,1,0:T(8,128)(2,1)} %tile.9), calls=%async_computation.1 | async-start | bytes 10616832 | tf_op jit(solution)/shard_map/all_to_all | solution.py:13
  46.2 105.3 %all_gather.19 = bf16[1,2304]{1,0:T(2,128)(2,1)S(1)} all-gather(bf16[1,1152]{1,0:T(2,128)(2,1)S(1)} %convert_element_type.61), channel_id=1, replica_groups=mesh['groups'=2,'seq'=4,'exp'=2,'tp'=2] {'exp'}, dimensions={1}, use_global_device_ids=true | all-gather | bytes 6912 | tf_op jit(solution)/shard_map/all_gather | solution.py:19
  151.6 10.3 %all-gather.6.cloned.1.call-done = bf16[1,1152,2304]{2,1,0:T(8,128)(2,1)} async-done(((bf16[1,1152,1152]{2,1,0:T(8,128)(2,1)}), bf16[1,1152,2304]{2,1,0:T(8,128)(2,1)}) %all-gather.6.cloned.1.call-update) | async-done | bytes 5308432 | tf_op jit(solution)/shard_map/all_gather | solution.py:19
  161.9 13.7 %convolution_convert_fusion = bf16[640,1152]{1,0:T(8,128)(2,1)} fusion(bf16[2304,1152]{1,0:T(8,128)(2,1)} %bitcast.10, bf16[640,1152]{1,0:T(8,128)(2,1)} %all-gather.4.cloned.1.call-done, bf16[1,1152,2304]{2,1,0:T(8,128)(2,1)} %all-gather.6.cloned.1.call-done, f32[2304]{0:T(1024)S(1)} %convert_reduce_fusion.1), kind=kOutput, calls=%fused_computation.33 | convolution fusion | flops 6810255360 | bytes 13575168 | tf_op jit(solution)/shard_map/dot_general | solution.py:111
  175.8 16.3 %all_gather.15 = bf16[1024,288]{0,1:T(8,128)(2,1)S(1)} all-gather(bf16[256,288]{0,1:T(8,128)(2,1)S(1)} %get-tuple-element.101), channel_id=1, replica_groups=mesh['groups'=2,'seq'=4,'exp'=2,'tp'=2] {'seq'}, dimensions={0}, use_global_device_ids=true | all-gather | bytes 737280 | tf_op jit(solution)/shard_map/all_gather | solution.py:38
  192.1 0.4 reshape.101
  192.5 0.9 copy.30
  193.4 15.5 %all_gather.16 = bf16[1024,288]{0,1:T(8,128)(2,1)S(1)} all-gather(bf16[256,288]{0,1:T(8,128)(2,1)S(1)} %get-tuple-element.100), channel_id=1, replica_groups=mesh['groups'=2,'seq'=4,'exp'=2,'tp'=2] {'seq'}, dimensions={0}, use_global_device_ids=true | all-gather | bytes 737280 | tf_op jit(solution)/shard_map/all_gather | solution.py:39
  209.0 0.4 reshape.103
  209.4 0.9 copy.31
  210.3 2.1 add_convert_fusion
  212.4 3.7 %all-to-all-start.2 = ((bf16[4,80,1152]{2,1,0:T(8,128)(2,1)}), bf16[4,80,1152]{2,1,0:T(8,128)(2,1)S(1)}, u32[]{:S(2)}, u32[]{:S(2)}) async-start(bf16[4,80,1152]{2,1,0:T(8,128)(2,1)} %bitcast.11), calls=%async_computation.3 | async-start | bytes 1474560 | tf_op jit(solution)/shard_map/all_to_all | solution.py:117
  216.1 6.3 %while.15 = (s32[]{:T(128)}, f32[4,256]{1,0:T(4,128)S(1)}, f32[4,256]{1,0:T(4,128)S(1)}, f32[4,256,72]{1,2,0:T(8,128)S(1)}, bf16[2,512,4,72]{1,3,2,0:T(8,128)(2,...) while((s32[]{:T(128)}, f32[4,256]{1,0:T(4,128)S(1)}, ...), condition=%wide.region_3.4_spmd.clone, body=%wide.region_0.3_spmd.clone.sunk | while | flops 155415552 | bytes 10044041 | solution.py:65
  216.1 1.5 bitcast_reduce_fusion.2
  217.7 0.4 fusion.50
  218.1 0.7 copy-done.1
  218.7 0.5 convolution_add_fusion.2
  219.3 1.5 bitcast_reduce_fusion.2
  220.8 0.4 fusion.50
  221.2 0.7 copy-done.1
  221.9 0.5 convolution_add_fusion.2
  222.7 0.7 divide_convert_fusion
  223.4 5.9 %all-to-all-done.2 = bf16[4,80,1152]{2,1,0:T(8,128)(2,1)S(1)} async-done(((bf16[4,80,1152]{2,1,0:T(8,128)(2,1)}), bf16[4,80,1152]{2,1,0:T(8,128)(2,1)S(1)}, u32[]{:S(2)}, u32[]{:S(2)}) %all-to-all-start.2) | async-done | bytes 737312 | tf_op jit(solution)/shard_map/all_to_all | solution.py:117
  229.3 1.3 gather_fusion
  230.6 0.6 reshape.110
  231.2 2.2 multiply_reduce_fusion
  (63 shorter events, 1.7 us)
Async XLA Ops:
  7.2 3.1 %copy-start = (bf16[128,1152]{1,0:T(8,128)(2,1)S(1)}, bf16[128,1152]{1,0:T(8,128)(2,1)}, u32[]{:S(2)}) copy-start(bf16[128,1152]{1,0:T(8,128)(2,1)} %param.21) | copy-start | bytes 884740
  7.2 144.4 %all-gather.4.cloned.1.call-start = ((), (), s32[]{:S(2)}) async-start(), calls=%async_computation.4 | async-start | bytes 2211840 | tf_op jit(solution)/shard_map/all_gather | solution.py:96
  10.6 26.4 %copy-start.2 = (bf16[1,1152,1152]{2,1,0:T(8,128)(2,1)S(1)}, bf16[1,1152,1152]{2,1,0:T(8,128)(2,1)}, u32[]{:S(2)}) copy-start(bf16[1,1152,1152]{2,1,0:T(8,128)(2,1)} %param.26) | copy-start | bytes 7962628
  36.2 125.6 %all-gather.6.cloned.1.call-start = ((), (), s32[]{:S(2)}) async-start(), calls=%async_computation.6 | async-start | bytes 7962624 | tf_op jit(solution)/shard_map/all_gather | solution.py:19
  39.8 6.4 %copy-start.7 = (f32[1,1152]{1,0:T(1,128)S(1)}, f32[1,1152]{1,0:T(1,128)}, u32[]{:S(2)}) copy-start(f32[1,1152]{1,0:T(1,128)} %param.25) | copy-start | bytes 13828
  39.8 111.8 %all-to-all-start.1 = ((bf16[2,1152,1152]{2,1,0:T(8,128)(2,1)}), bf16[2,1152,1152]{2,1,0:T(8,128)(2,1)}, u32[]{:S(2)}, u32[]{:S(2)}) async-start(bf16[2,1152,1152]{2,1,0:T(8,128)(2,1)} %tile.9), calls=%async_computation.1 | async-start | bytes 10616832 | tf_op jit(solution)/shard_map/all_to_all | solution.py:13
  46.1 164.2 %reduce-scatter.2.cloned.1.call-start = ((), (), s32[]{:S(2)}) async-start(), calls=%async_computation.5 | async-start | bytes 2211840 | tf_op jit(solution)/shard_map/reduce_scatter | solution.py:110
  161.8 13.8 %copy-start.10 = (s32[2]{0:T(128)S(1)}, s32[2]{0:T(128)}, u32[]{:S(2)}) copy-start(s32[2]{0:T(128)} %param.20) | copy-start | bytes 28
  161.8 13.9 %copy-start.3 = (bf16[256,288]{0,1:T(8,128)(2,1)S(1)}, bf16[256,288]{0,1:T(8,128)(2,1)}, u32[]{:S(2)}) copy-start(bf16[256,288]{0,1:T(8,128)(2,1)} %param.17) | copy-start | bytes 442372
  161.9 13.9 %copy-start.4 = (bf16[256,288]{0,1:T(8,128)(2,1)S(1)}, bf16[256,288]{0,1:T(8,128)(2,1)}, u32[]{:S(2)}) copy-start(bf16[256,288]{0,1:T(8,128)(2,1)} %param.19) | copy-start | bytes 442372
  161.9 13.9 %copy-start.5 = (bf16[256,288]{0,1:T(8,128)(2,1)S(1)}, bf16[256,288]{0,1:T(8,128)(2,1)}, u32[]{:S(2)}) copy-start(bf16[256,288]{0,1:T(8,128)(2,1)} %param.16) | copy-start | bytes 442372
  161.9 13.9 %copy-start.6 = (bf16[256,288]{0,1:T(8,128)(2,1)S(1)}, bf16[256,288]{0,1:T(8,128)(2,1)}, u32[]{:S(2)}) copy-start(bf16[256,288]{0,1:T(8,128)(2,1)} %param.18) | copy-start | bytes 442372
  192.5 17.8 %copy-start.8 = (f32[1,1152]{1,0:T(1,128)S(1)}, f32[1,1152]{1,0:T(1,128)}, u32[]{:S(2)}) copy-start(f32[1,1152]{1,0:T(1,128)} %param.27) | copy-start | bytes 13828
  212.4 16.9 %all-to-all-start.2 = ((bf16[4,80,1152]{2,1,0:T(8,128)(2,1)}), bf16[4,80,1152]{2,1,0:T(8,128)(2,1)S(1)}, u32[]{:S(2)}, u32[]{:S(2)}) async-start(bf16[4,80,1152]{2,1,0:T(8,128)(2,1)} %bitcast.11), calls=%async_computation.3 | async-start | bytes 1474560 | tf_op jit(solution)/shard_map/all_to_all | solution.py:117
  216.1 6.4 %copy-start.9 = (f32[128,2]{0,1:T(2,128)S(1)}, f32[128,2]{0,1:T(2,128)}, u32[]{:S(2)}) copy-start(f32[128,2]{0,1:T(2,128)} %param.23) | copy-start | bytes 3076
  217.7 1.1 copy-start.1
  220.8 1.1 copy-start.1
Sparse Core Ops, SparseCore 0:
  36.4 8.7 all-gather.3
  46.7 115.0 all-gather.5
  175.7 7.4 reduce-scatter.1
